TPU v7x, 32 devices: a whole 2x2x4 slice. The times are simulated.
32 devices in a mesh: lon: 8 (over y, x, core), lat: 4 (over z).
Axes of the slice: x: 2, y: 2, z: 4, core: 2. Of those that a mesh axis runs over, the one named last changes fastest.
Arguments:
- grid_latent: bfloat16 [4, 8, 1024, 512], P('lat', 'lon'), may hold values from -6 to 6
- mesh_latent: bfloat16 [4, 8, 160, 512], P('lat', 'lon'), may hold values from -6 to 6
- edge_geometry: float32 [4, 8, 4, 2048], P('lat', 'lon'), may hold values from -6 to 6
- senders: int32 [4, 8, 2048], P('lat', 'lon'), may hold values from 0 to 1023
- receivers: int32 [4, 8, 2048], P('lat', 'lon'), may hold values from 0 to 1439, as said below
- w_grid: bfloat16 [512, 512], replicated, may hold values from -0.25 to 0.25
- w_mesh: bfloat16 [512, 512], replicated, may hold values from -0.25 to 0.25
- w_edge: float32 [4, 512], replicated, may hold values from -3 to 3
- edge_bias: float32 [512], replicated, may hold values from -3 to 3
- w_message: bfloat16 [512, 512], replicated, may hold values from -0.25 to 0.25
- w_node: bfloat16 [1024, 512], replicated, may hold values from -0.1875 to 0.1875
- w_output: bfloat16 [512, 512], replicated, may hold values from -0.25 to 0.25
- norm_gain: float32 [512], replicated, may hold values from 0.1 to 1.9
- norm_bias: float32 [512], replicated, may hold values from -3 to 3
Outputs:
- mesh_out: bfloat16 [4, 8, 160, 512], P('lat', 'lon')
Inputs may be any that keep to these rules, and one draw needn't show every extreme that they name: `receivers`: r // 160 is a neighbour slot s from 0 to 8 (latitude offset s // 3 - 1, longitude offset s % 3 - 1); edges of the first band never name latitude offset -1, those of the last band never +1. For s other than 4, with k = s for s < 4 and k = s - 1 otherwise, the row r % 160 lies in k * 16 to k * 16 + 15 for s = 1, 3, 5, 7 and in k * 16 to k * 16 + 3 for s = 0, 2, 6, 8.
All inputs are finite; a program needn't handle non-finite values.
Results may differ from a plain program's by a relative error of at most 0.0095.
Values may be sent and summed in bfloat16 or wider, within the bound.
A program may use at most 64 MiB of HBM per device.

v0:
```python
import functools

import jax
import jax.numpy as jnp
from jax import lax
from jax.experimental import pallas as pl
from jax.experimental.pallas import tpu as pltpu
from jax.sharding import PartitionSpec as P

B_SIDE = 16
B_CORNER = 4
TAIL = 16
OFFER_AT = 0
MESH = pl.DeviceIdType.MESH

BF16 = jnp.bfloat16
F32 = jnp.float32

STRIPS = tuple((s, s if s < 4 else s - 1) for s in range(9) if s != 4)
SIDES = (1, 3, 5, 7)
CORNERS = (0, 2, 6, 8)


def nt(a, b):
    return lax.dot_general(a, b, (((1,), (1,)), ((), ())), preferred_element_type=F32)


def nn(a, b):
    return jnp.dot(a, b, preferred_element_type=F32)


def halves(x):
    high = x.astype(BF16)
    return high, (x - high.astype(F32)).astype(BF16)


def kernel(
    n_lon,
    n_lat,
    grid_h,
    mesh_h,
    geo_h,
    snd_h,
    rcv_h,
    w_grid_h,
    w_mesh_h,
    w_edge_h,
    bias_h,
    w_message_h,
    w_node_h,
    w_output_h,
    gain_h,
    nbias_h,
    out_ref,
    grid_v,
    mesh_v,
    geo_v,
    snd_v,
    rcv_v,
    w_grid_v,
    w_mesh_v,
    w_edge_v,
    bias_v,
    w_message_v,
    w_node_v,
    w_output_v,
    gain_v,
    nbias_v,
    table,
    onehot,
    from_grid,
    summed,
    got_mesh,
    put_sum,
    got_sum,
    load_sem,
    send_a,
    recv_a,
    send_b,
    recv_b,
):
    lon = lax.axis_index("lon")
    lat = lax.axis_index("lat")
    rows, features = mesh_v.shape
    grid_rows = grid_v.shape[0]
    edges = snd_v.shape[1]
    side_base = rows
    corner_base = rows + 4 * B_SIDE
    slots = corner_base + 4 * B_CORNER

    sources = [
        (snd_h.at[0], snd_v),
        (w_grid_h, w_grid_v),
        (grid_h.at[0, 0], grid_v),
        (mesh_h.at[0, 0], mesh_v),
        (rcv_h.at[0], rcv_v),
        (geo_h.at[0, 0], geo_v),
        (w_edge_h, w_edge_v),
        (bias_h, bias_v),
        (w_mesh_h, w_mesh_v),
        (w_node_h, w_node_v),
        (w_message_h, w_message_v),
        (w_output_h, w_output_v),
        (gain_h, gain_v),
        (nbias_h, nbias_v),
    ]
    loads = {}
    for number, (source, target) in enumerate(sources):
        copy = pltpu.make_async_copy(source, target, load_sem.at[number])
        copy.start()
        loads[id(target)] = copy

    def loaded(ref):
        loads[id(ref)].wait()

    def there(dlat, dlon):
        return {
            "lat": lat + dlat,
            "lon": lax.rem(lon + dlon + n_lon, n_lon),
        }

    def has(dlat):
        if dlat == 0:
            return None
        return lat > 0 if dlat < 0 else lat < n_lat - 1

    def guarded(dlat, body, other=None):
        condition = has(dlat)
        if condition is None:
            body()
            return
        pl.when(condition)(body)
        if other is not None:
            pl.when(jnp.logical_not(condition))(other)

    barrier = pltpu.get_barrier_semaphore()
    for dlat in (0, -1, 1):

        def greet(dlat=dlat):
            for dlon in (-1, 0, 1):
                if (dlat, dlon) != (0, 0):
                    pl.semaphore_signal(
                        barrier, inc=1, device_id=there(dlat, dlon), device_id_type=MESH
                    )

        guarded(dlat, greet)

    def size_of(slot):
        return B_SIDE if slot in SIDES else B_CORNER

    def mesh_copy(slot, k):
        return pltpu.make_async_remote_copy(
            src_ref=mesh_v.at[pl.ds(k * B_SIDE, size_of(slot))],
            dst_ref=got_mesh.at[k, pl.ds(0, size_of(slot))],
            send_sem=send_a.at[k],
            recv_sem=recv_a.at[k],
            device_id=there(-(slot // 3 - 1), -(slot % 3 - 1)),
            device_id_type=MESH,
        )

    def sum_copy(slot, k):
        return pltpu.make_async_remote_copy(
            src_ref=put_sum.at[k, pl.ds(0, size_of(slot))],
            dst_ref=got_sum.at[k, pl.ds(0, size_of(slot))],
            send_sem=send_b.at[k],
            recv_sem=recv_b.at[k],
            device_id=there(slot // 3 - 1, slot % 3 - 1),
            device_id_type=MESH,
        )

    def in_band(dlat):
        return [(s, k) for s, k in STRIPS if s // 3 - 1 == dlat]

    def offer_strips():
        arrivals = 2 + 3 * (lat > 0).astype(jnp.int32) + 3 * (lat < n_lat - 1).astype(jnp.int32)
        pl.semaphore_wait(barrier, arrivals)
        for dlat in (-1, 1, 0):

            def send(dlat=dlat):
                for s, k in in_band(dlat):
                    mesh_copy(s, k).start()

            guarded(-dlat, send)

    step = min(512, edges)
    starts = list(range(0, edges, step))
    loaded(snd_v)
    for start in starts:
        span = pl.ds(start, step)
        ids = lax.broadcasted_iota(jnp.int32, (grid_rows, step), 0)
        onehot[:grid_rows, span] = jnp.where(ids == snd_v[:, span], 1.0, 0.0).astype(BF16)
    loaded(w_grid_v)
    w_grid_t = jnp.transpose(w_grid_v[...])
    loaded(grid_v)
    table[:, :grid_rows] = (0.5 * nt(w_grid_t, grid_v[...])).astype(BF16)
    loaded(mesh_v)
    for number, start in enumerate(starts):
        if number == OFFER_AT:
            offer_strips()
        span = pl.ds(start, step)
        from_grid[:, span] = nn(table[:, :grid_rows], onehot[:grid_rows, span])
    if OFFER_AT >= len(starts):
        offer_strips()

    loaded(rcv_v)
    loaded(geo_v)
    picks = rcv_v[...]
    shift, spot = 0, picks
    for s in range(9):
        k = s if s < 4 else s - 1
        if s == 4:
            base = -4 * rows
        elif s in SIDES:
            base = side_base + B_SIDE * SIDES.index(s) - k * B_SIDE - s * rows
        else:
            base = corner_base + B_CORNER * CORNERS.index(s) - k * B_SIDE - s * rows
        if s == 0:
            spot = spot + base
        else:
            spot = spot + jnp.where(picks >= s * rows, base - shift, 0)
        shift = base
    for start in starts:
        span = pl.ds(start, step)
        ids = lax.broadcasted_iota(jnp.int32, (slots, step), 0)
        onehot[grid_rows : grid_rows + slots, span] = jnp.where(
            ids == spot[:, start : start + step], 1.0, 0.0
        ).astype(BF16)
    high, low = [part.astype(F32) for part in halves(geo_v[...])]
    ones = jnp.ones((2, edges), F32)
    zeros = jnp.zeros((2, edges), F32)
    onehot[grid_rows + slots :, :] = jnp.concatenate([high, high, low, ones, zeros], 0).astype(BF16)

    loaded(w_edge_v)
    loaded(bias_v)
    high, low = [part.astype(F32) for part in halves(w_edge_v[...])]
    bias_high, bias_low = [part.astype(F32) for part in halves(bias_v[...])]
    tail = jnp.concatenate(
        [high, low, high, bias_high, bias_low, jnp.zeros((2, features), F32)], 0
    )
    loaded(w_mesh_v)
    loaded(w_node_v)
    loaded(w_message_v)
    loaded(w_output_v)
    loaded(gain_v)
    loaded(nbias_v)
    node_own = nn(mesh_v[...], w_node_v[:features, :])

    for dlat in (-1, 0, 1):

        def arrive(dlat=dlat):
            for s, k in in_band(dlat):
                mesh_copy(s, k).wait_recv()

        def nothing(dlat=dlat):
            for s, k in in_band(dlat):
                got_mesh[k] = jnp.zeros(got_mesh.shape[1:], BF16)

        guarded(dlat, arrive, nothing)

    strip = dict(STRIPS)
    corners = jnp.concatenate(
        [got_mesh[strip[s]].astype(F32)[:B_CORNER] for s in CORNERS], 0
    ).astype(BF16)
    mesh_all = jnp.concatenate(
        [mesh_v[...]] + [got_mesh[strip[s]] for s in SIDES] + [corners], 0
    )
    mesh_table = jnp.concatenate([nn(mesh_all, w_mesh_v[...]), tail], 0) * 0.5
    table[:, grid_rows:] = jnp.transpose(mesh_table).astype(BF16)

    for start in range(0, edges, step):
        span = pl.ds(start, step)
        half = from_grid[:, span] + nn(table[:, grid_rows:], onehot[grid_rows:, span])
        hidden = (half + half * jnp.tanh(half)).astype(BF16)
        added = nt(onehot[grid_rows:, span], hidden)
        if start == 0:
            summed[...] = added
        else:
            summed[...] += added

    for s in SIDES:
        first = side_base + B_SIDE * SIDES.index(s)
        put_sum[strip[s]] = summed[first : first + B_SIDE, :].astype(BF16)
    for s in CORNERS:
        first = corner_base + B_CORNER * CORNERS.index(s)
        part = summed[first : first + B_CORNER, :]
        rest = jnp.zeros((B_SIDE - B_CORNER, features), F32)
        put_sum[strip[s]] = jnp.concatenate([part, rest], 0).astype(BF16)
    for dlat in (-1, 1, 0):

        def send(dlat=dlat):
            for s, k in in_band(dlat):
                sum_copy(s, k).start()

        guarded(dlat, send)

    high, low = halves(summed[:rows, :])
    own_message = nn(high, w_message_v[...]) + nn(low, w_message_v[...])
    for dlat in (-1, 0, 1):

        def arrive(dlat=dlat):
            for s, k in in_band(dlat):
                sum_copy(s, k).wait_recv()

        def nothing(dlat=dlat):
            for s, k in in_band(dlat):
                got_sum[k] = jnp.zeros(got_sum.shape[1:], BF16)

        guarded(-dlat, arrive, nothing)

    border = 8 * B_SIDE
    pieces = []
    for s, k in STRIPS:
        piece = got_sum[k]
        if s in CORNERS:
            rest = jnp.zeros((B_SIDE - B_CORNER, features), F32)
            piece = jnp.concatenate([piece.astype(F32)[:B_CORNER], rest], 0).astype(BF16)
        pieces.append(piece)
    border_message = nn(jnp.concatenate(pieces, 0), w_message_v[...])
    gathered = jnp.concatenate(
        [own_message[:border] + border_message, own_message[border:]], 0
    )
    node = node_own + nn(gathered.astype(BF16), w_node_v[features:, :])
    node_hidden = (node * jax.nn.sigmoid(node)).astype(BF16)
    update = nn(node_hidden, w_output_v[...])
    row_mean = jnp.mean(update, axis=-1, keepdims=True)
    centered = update - row_mean
    row_var = jnp.mean(centered * centered, axis=-1, keepdims=True)
    normed = centered * lax.rsqrt(row_var + 1e-05) * gain_v[...] + nbias_v[...]
    out_ref[0, 0] = (mesh_v[...].astype(F32) + normed).astype(BF16)

    for dlat in (-1, 0, 1):

        def sent(dlat=dlat):
            for s, k in in_band(dlat):
                mesh_copy(s, k).wait_send()

        def sent_sum(dlat=dlat):
            for s, k in in_band(dlat):
                sum_copy(s, k).wait_send()

        guarded(-dlat, sent)
        guarded(dlat, sent_sum)


def local(n_lon, n_lat, *args):
    args = [a.reshape(1, -1) if a.ndim == 1 else a for a in args]
    grid_latent, mesh_latent, geometry, senders = args[:4]
    rows, features = mesh_latent.shape[2:]
    grid_rows = grid_latent.shape[2]
    edges = senders.shape[2]
    slots = rows + 4 * B_SIDE + 4 * B_CORNER
    wide = grid_rows + slots + TAIL
    loads = []
    for number, a in enumerate(args):
        shape = a.shape[2:] if number < 3 else a.shape[1:] if number < 5 else a.shape
        loads.append(pltpu.VMEM(shape, a.dtype))
    return pl.pallas_call(
        functools.partial(kernel, n_lon, n_lat),
        out_shape=pltpu.VMEM(mesh_latent.shape, BF16),
        in_specs=[pl.BlockSpec(memory_space=pl.ANY)] * len(args),
        out_specs=pl.BlockSpec(memory_space=pltpu.VMEM),
        scratch_shapes=loads
        + [
            pltpu.VMEM((features, wide), BF16),
            pltpu.VMEM((wide, edges), BF16),
            pltpu.VMEM((features, edges), F32),
            pltpu.VMEM((slots + TAIL, features), F32),
            pltpu.VMEM((8, B_SIDE, features), BF16),
            pltpu.VMEM((8, B_SIDE, features), BF16),
            pltpu.VMEM((8, B_SIDE, features), BF16),
            pltpu.SemaphoreType.DMA((len(args),)),
            pltpu.SemaphoreType.DMA((8,)),
            pltpu.SemaphoreType.DMA((8,)),
            pltpu.SemaphoreType.DMA((8,)),
            pltpu.SemaphoreType.DMA((8,)),
        ],
        compiler_params=pltpu.CompilerParams(
            collective_id=0, has_side_effects=True, vmem_limit_bytes=56 * 1024 * 1024
        ),
    )(*args)


def solution(mesh):
    return jax.shard_map(
        functools.partial(local, mesh.shape["lon"], mesh.shape["lat"]),
        mesh=mesh,
        in_specs=(
            P("lat", "lon", None, None),
            P("lat", "lon", None, None),
            P("lat", "lon", None, None),
            P("lat", "lon", None),
            P("lat", "lon", None),
            P(),
            P(),
            P(),
            P(),
            P(),
            P(),
            P(),
            P(),
            P(),
        ),
        out_specs=P("lat", "lon", None, None),
        check_vma=False,
    )
```

profile of v0, /device:TPU:0, one launch (start us, length us, event | category | flops | bytes accessed | tf_op | source)
XLA Modules:
  0.0 16.1 jit_solution(1291902422683583846)
XLA Ops:
  0.0 15.4 %shard_map.136 = bf16[1,1,160,512]{3,2,1,0:T(8,128)(2,1)S(1)} custom-call(bf16[1,1,1024,512]{3,2,1,0:T(8,128)(2,1)} %grid_h.1, bf16[1,1,160,512]{3,2,1,0:T(8,128)(2,1)} %mesh_h.1, f32[1,1,4,2048]{3,2,1,0:T(4,128)} %geo_h.1, s32[1,1,2048]{2,1,0:T(1,128)} %snd_h.1, s32[1,1,2048]{2,1,0:T(1,128)} %rcv_h.1, bf16[512,512]{1,0:T(8,128)(2,1)} %w_grid_h.1, ...), custom_call_target="tpu_custom_call" | custom-call | tf_op jit(solution)/shard_map/pallas_call | solution.py:357
  15.4 0.7 %copy.16 = bf16[1,1,160,512]{3,2,1,0:T(8,128)(2,1)} copy(bf16[1,1,160,512]{3,2,1,0:T(8,128)(2,1)S(1)} %shard_map.136) | data formatting | bytes 327680
where the time goes:
time: 16.2 us; the launch traced here: 16.1 us
  Pallas kernels  15.4 us (95%)
  local copies, waits for them, and re-layouts  0.67 us (4%)
    pallas_call x1, Pallas kernels, local(): pl.pallas_call(functools.partial(kernel, n_lon, n_lat), out_shape=pltpu.V...  15.4 us
    unnamed x1, local copies, waits for them, and re-layouts  0.67 us

commit v1 on v0

v1 whole, which is shorter than its diff:
```python
import functools

import jax
import jax.numpy as jnp
from jax import lax
from jax.experimental import pallas as pl
from jax.experimental.pallas import tpu as pltpu
from jax.sharding import PartitionSpec as P

B_SIDE = 16
B_CORNER = 4
BLOCK = 8
LANES = 128
DIGIT = 256
CHUNK = 512
SIDES_AT = 0
CORNERS_AT = 1
MESH = pl.DeviceIdType.MESH

BF16 = jnp.bfloat16
F32 = jnp.float32

SIDES = (1, 3, 5, 7)
CORNERS = (0, 2, 6, 8)


def strip(slot):
    return slot if slot < 4 else slot - 1


def nn(a, b):
    return jnp.dot(a, b, preferred_element_type=F32)


def halves(x):
    high = x.astype(BF16)
    return high, (x - high.astype(F32)).astype(BF16)


def down(row, count):
    return jnp.transpose(jnp.broadcast_to(row, (count, row.shape[1])))


def equal(a, b):
    one = jnp.ones(a.shape, BF16)
    return jnp.where(a == b, one, jnp.zeros_like(one))


def kernel(
    n_lon,
    n_lat,
    grid_h,
    mesh_h,
    geo_h,
    snd_h,
    rcv_h,
    w_grid_h,
    w_mesh_h,
    w_edge_h,
    bias_h,
    w_message_h,
    w_node_h,
    w_output_h,
    gain_h,
    nbias_h,
    out_ref,
    grid_v,
    mesh_v,
    geo_v,
    snd_v,
    rcv_v,
    w_grid_v,
    w_mesh_v,
    w_edge_v,
    bias_v,
    w_message_v,
    w_node_v,
    w_output_v,
    gain_v,
    nbias_v,
    table,
    edge_table,
    picks_e,
    picks_n,
    before,
    put_sum,
    got_sum,
    load_sem,
    send_sem,
    recv_sem,
    ready_sem,
):
    lon = lax.axis_index("lon")
    lat = lax.axis_index("lat")
    rows, features = mesh_v.shape
    grid_rows = grid_v.shape[0]
    edges = snd_v.shape[1]
    corner_base = rows + 4 * B_SIDE
    slots = corner_base + 4 * BLOCK
    cut = rows // LANES * LANES
    border = 8 * B_SIDE

    def there(dlat, dlon):
        return {
            "lat": lat + dlat,
            "lon": lax.rem(lon + dlon + n_lon, n_lon),
        }

    def guarded(dlat, body):
        if dlat == 0:
            body()
        else:
            pl.when(lat > 0 if dlat < 0 else lat < n_lat - 1)(body)

    groups = [
        [(snd_h.at[0], snd_v)],
        [(w_grid_h, w_grid_v), (grid_h.at[0, 0], grid_v)],
        [
            (mesh_h.at[0, 0], mesh_v),
            (w_mesh_h, w_mesh_v),
            (rcv_h.at[0], rcv_v),
            (geo_h.at[0, 0], geo_v),
            (w_edge_h, w_edge_v),
        ],
        [(bias_h, bias_v), (gain_h, gain_v), (nbias_h, nbias_v)],
        [(w_message_h, w_message_v), (w_node_h, w_node_v), (w_output_h, w_output_v)],
    ]
    for number, group in enumerate(groups):
        for source, target in group:
            pltpu.make_async_copy(source, target, load_sem.at[number]).start()

    def bytes_of(ref):
        return ref.dtype.itemsize * functools.reduce(lambda a, b: a * b, ref.shape)

    def span_of(total):
        if total < bytes_of(snd_v):
            return snd_v.at[:, pl.ds(0, total // snd_v.dtype.itemsize)]
        if total < bytes_of(table):
            return table.at[pl.ds(0, total // (2 * features))]
        return before.at[pl.ds(0, total // (4 * features))]

    def loaded(number):
        view = span_of(sum(bytes_of(target) for _, target in groups[number]))
        pltpu.make_async_copy(view, view, load_sem.at[number]).wait()

    edge_table[...] = jnp.zeros(edge_table.shape, BF16)
    got_sum[...] = jnp.zeros(got_sum.shape, BF16)

    barrier = pltpu.get_barrier_semaphore()

    def greet(dlat, dlon):
        pl.semaphore_signal(barrier, inc=1, device_id=there(dlat, dlon), device_id_type=MESH)

    greet(0, -1)
    greet(0, 1)
    guarded(-1, lambda: greet(-1, 0))
    guarded(1, lambda: greet(1, 0))

    def offset(slot):
        return slot // 3 - 1, slot % 3 - 1

    def place(slot):
        if slot in SIDES:
            return rows + B_SIDE * SIDES.index(slot)
        return corner_base + BLOCK * CORNERS.index(slot)

    def size_of(slot):
        return B_SIDE if slot in SIDES else B_CORNER

    def mesh_copy(slot):
        dlat, dlon = offset(slot)
        size = size_of(slot)
        return pltpu.make_async_remote_copy(
            src_ref=table.at[pl.ds(grid_rows + strip(slot) * B_SIDE, size)],
            dst_ref=edge_table.at[pl.ds(place(slot) - cut, size)],
            send_sem=send_sem.at[1 - dlat],
            recv_sem=recv_sem.at[1 + dlat],
            device_id=there(-dlat, -dlon),
            device_id_type=MESH,
        )

    def sum_copy(slot):
        dlat, dlon = offset(slot)
        size = size_of(slot)
        return pltpu.make_async_remote_copy(
            src_ref=put_sum.at[pl.ds(place(slot) - rows, size)],
            dst_ref=got_sum.at[pl.ds(strip(slot) * B_SIDE, size)],
            send_sem=send_sem.at[4 + dlat],
            recv_sem=recv_sem.at[4 - dlat],
            device_id=there(dlat, dlon),
            device_id_type=MESH,
        )

    def settle(sems, first):
        for dlat in (-1, 1, 0):

            def body(dlat=dlat):
                count = sum(size_of(s) for s in SIDES + CORNERS if offset(s)[0] == dlat)
                view = table.at[pl.ds(0, count)]
                pltpu.make_async_copy(view, view, sems.at[first + 1 + dlat]).wait()

            guarded(dlat, body)

    def each(chosen, sign, action):
        for dlat in (-1, 1, 0):
            members = [s for s in chosen if offset(s)[0] == sign * dlat]
            if members:

                def body(members=members):
                    for s in members:
                        action(s)

                guarded(dlat, body)

    def send_sides():
        arrivals = 2 + (lat > 0).astype(jnp.int32) + (lat < n_lat - 1).astype(jnp.int32)
        pl.semaphore_wait(barrier, arrivals)
        each(SIDES, -1, lambda s: mesh_copy(s).start())
        for dlat in (-1, 1):

            def tell(dlat=dlat):
                pl.semaphore_signal(
                    ready_sem.at[0 if dlat > 0 else 1],
                    inc=1,
                    device_id=there(dlat, 0),
                    device_id_type=MESH,
                )

            guarded(dlat, tell)

    def send_corners():
        for dlat in (-1, 1):

            def go(dlat=dlat):
                pl.semaphore_wait(ready_sem.at[0 if dlat < 0 else 1], 1)
                for s in CORNERS:
                    if offset(s)[0] == -dlat:
                        mesh_copy(s).start()

            guarded(dlat, go)

    step = min(CHUNK, edges)
    starts = list(range(0, edges, step))
    digits = grid_rows // DIGIT
    lane = lax.broadcasted_iota(jnp.int32, (step, LANES), 1).astype(F32)
    lanes = [(lane + float(LANES * h)).astype(BF16) for h in range(DIGIT // LANES)]

    loaded(0)
    senders = snd_v[...]
    upper = lax.shift_left(lax.shift_right_logical(senders, 8), 8)
    lower = (senders - upper).astype(F32).astype(BF16)
    upper = upper.astype(F32).astype(BF16)
    loaded(1)
    table[:grid_rows, :] = (0.5 * nn(grid_v[...], w_grid_v[...])).astype(BF16)
    for start in starts:
        span = pl.ds(start, step)
        low = down(lower[:, start : start + step], LANES)
        high = down(upper[:, start : start + step], LANES)
        for q in range(digits):
            digit = (high - float(DIGIT * q)) + low
            for h in range(DIGIT // LANES):
                picks_e[span, pl.ds(q * DIGIT + h * LANES, LANES)] = equal(digit, lanes[h])

    loaded(2)
    loaded(3)
    high, low = [part.astype(F32) for part in halves(w_edge_v[...])]
    bias_high, bias_low = [part.astype(F32) for part in halves(bias_v[...])]
    blank = jnp.zeros((BLOCK - B_CORNER, features), F32)
    last = jnp.concatenate(
        [bias_high, bias_low, jnp.zeros((B_CORNER - 2, features), F32)], 0
    )
    own = nn(mesh_v[...], w_mesh_v[...])
    table[grid_rows:, :] = (
        0.5
        * jnp.concatenate(
            [own, jnp.zeros((corner_base - rows, features), F32)]
            + [blank, high, blank, low, blank, high, blank, last],
            0,
        )
    ).astype(BF16)

    picks = rcv_v[...]
    shift, spot = 0, picks
    for s in range(9):
        base = (0 if s == 4 else place(s) - strip(s) * B_SIDE) - s * rows
        if s == 0:
            spot = spot + base
        else:
            spot = spot + jnp.where(picks >= s * rows, base - shift, 0)
        shift = base
    spot = spot.astype(F32).astype(BF16)
    high, low = [part.astype(F32) for part in halves(geo_v[...])]
    empty = jnp.zeros((BLOCK - B_CORNER, edges), F32)
    ones = jnp.concatenate([jnp.ones((2, edges), F32), jnp.zeros((2, edges), F32)], 0)
    tail = jnp.concatenate(
        [jnp.zeros((corner_base - cut, edges), F32)]
        + [empty, high, empty, high, empty, low, empty, ones],
        0,
    ).astype(BF16)
    for start in starts:
        span = pl.ds(start, step)
        at = down(spot[:, start : start + step], LANES)
        for h in range(slots // LANES):
            found = equal(at, lanes[h])
            if h * LANES == cut:
                found = found + jnp.transpose(tail[:, start : start + step])
            picks_e[span, pl.ds(grid_rows + h * LANES, LANES)] = found
    row = lax.broadcasted_iota(jnp.int32, (slots, step), 0).astype(F32).astype(BF16)
    for start in starts:
        at = jnp.broadcast_to(spot[:, start : start + step], (slots, step))
        picks_n[:, pl.ds(start, step)] = equal(row, at)

    for number, start in enumerate(starts):
        if number == SIDES_AT:
            send_sides()
        if number == CORNERS_AT:
            send_corners()
        span = pl.ds(start, step)
        before[span, :] = nn(picks_e[span, :], table[...])

    settle(recv_sem, 0)

    summed = None
    for start in starts:
        span = pl.ds(start, step)
        half = before[span, :] + nn(picks_e[span, grid_rows + cut :], edge_table[...])
        hidden = (half + half * jnp.tanh(half)).astype(BF16)
        added = nn(picks_n[:, span], hidden)
        summed = added if summed is None else summed + added

    put_sum[...] = summed[rows:, :].astype(BF16)
    each(SIDES + CORNERS, 1, lambda s: sum_copy(s).start())

    loaded(4)
    fold = nn(w_message_v[...], w_node_v[features:, :]).astype(BF16)
    high, low = halves(summed[:rows, :])
    node = nn(mesh_v[...], w_node_v[:features, :]) + nn(high, fold) + nn(low, fold)

    def finish(node, span):
        node_hidden = (node * jax.nn.sigmoid(node)).astype(BF16)
        update = nn(node_hidden, w_output_v[...])
        row_mean = jnp.mean(update, axis=-1, keepdims=True)
        centered = update - row_mean
        row_var = jnp.mean(centered * centered, axis=-1, keepdims=True)
        normed = centered * lax.rsqrt(row_var + 1e-05) * gain_v[...] + nbias_v[...]
        out_ref[0, 0, span, :] = (mesh_v[span, :].astype(F32) + normed).astype(BF16)

    finish(node[border:], pl.ds(border, rows - border))
    settle(recv_sem, 3)
    finish(node[:border] + nn(got_sum[...], fold), pl.ds(0, border))

    settle(send_sem, 0)
    settle(send_sem, 3)


def local(n_lon, n_lat, *args):
    args = [a.reshape(1, -1) if a.ndim == 1 else a for a in args]
    grid_latent, mesh_latent, geometry, senders = args[:4]
    rows, features = mesh_latent.shape[2:]
    grid_rows = grid_latent.shape[2]
    edges = senders.shape[2]
    slots = rows + 4 * B_SIDE + 4 * BLOCK
    cut = rows // LANES * LANES
    loads = []
    for number, a in enumerate(args):
        shape = a.shape[2:] if number < 3 else a.shape[1:] if number < 5 else a.shape
        loads.append(pltpu.VMEM(shape, a.dtype))
    return pl.pallas_call(
        functools.partial(kernel, n_lon, n_lat),
        out_shape=pltpu.VMEM(mesh_latent.shape, BF16),
        in_specs=[pl.BlockSpec(memory_space=pl.ANY)] * len(args),
        out_specs=pl.BlockSpec(memory_space=pltpu.VMEM),
        scratch_shapes=loads
        + [
            pltpu.VMEM((grid_rows + slots, features), BF16),
            pltpu.VMEM((slots - cut, features), BF16),
            pltpu.VMEM((edges, grid_rows + slots), BF16),
            pltpu.VMEM((slots, edges), BF16),
            pltpu.VMEM((edges, features), F32),
            pltpu.VMEM((slots - rows, features), BF16),
            pltpu.VMEM((8 * B_SIDE, features), BF16),
            pltpu.SemaphoreType.DMA((5,)),
            pltpu.SemaphoreType.DMA((6,)),
            pltpu.SemaphoreType.DMA((6,)),
            pltpu.SemaphoreType.REGULAR((2,)),
        ],
        compiler_params=pltpu.CompilerParams(
            collective_id=0, has_side_effects=True, vmem_limit_bytes=56 * 1024 * 1024
        ),
    )(*args)


def solution(mesh):
    return jax.shard_map(
        functools.partial(local, mesh.shape["lon"], mesh.shape["lat"]),
        mesh=mesh,
        in_specs=(
            P("lat", "lon", None, None),
            P("lat", "lon", None, None),
            P("lat", "lon", None, None),
            P("lat", "lon", None),
            P("lat", "lon", None),
            P(),
            P(),
            P(),
            P(),
            P(),
            P(),
            P(),
            P(),
            P(),
        ),
        out_specs=P("lat", "lon", None, None),
        check_vma=False,
    )
```

time: 16.2 us -> 16.2 us (level)
  no operation moved by 1% of the time
where the time goes in v1:
time: 16.2 us; the launch traced here: 16 us
  Pallas kernels  15.4 us (95%)
  local copies, waits for them, and re-layouts  0.67 us (4%)
    pallas_call x1, Pallas kernels, local(): pl.pallas_call(functools.partial(kernel, n_lon, n_lat), out_shape=pltpu.V...  15.4 us
    unnamed x1, local copies, waits for them, and re-layouts  0.67 us

profile of v1, /device:TPU:0, one launch (start us, length us, event | category | flops | bytes accessed | tf_op | source)
XLA Modules:
  0.0 16.0 jit_solution(16267259713869801192)
XLA Ops:
  0.0 15.4 %shard_map.136 = bf16[1,1,160,512]{3,2,1,0:T(8,128)(2,1)S(1)} custom-call(bf16[1,1,1024,512]{3,2,1,0:T(8,128)(2,1)} %grid_h.1, bf16[1,1,160,512]{3,2,1,0:T(8,128)(2,1)} %mesh_h.1, f32[1,1,4,2048]{3,2,1,0:T(4,128)} %geo_h.1, s32[1,1,2048]{2,1,0:T(1,128)} %snd_h.1, s32[1,1,2048]{2,1,0:T(1,128)} %rcv_h.1, bf16[512,512]{1,0:T(8,128)(2,1)} %w_grid_h.1, ...), custom_call_target="tpu_custom_call" | custom-call | tf_op jit(solution)/shard_map/pallas_call | solution.py:368
  15.4 0.7 %copy.16 = bf16[1,1,160,512]{3,2,1,0:T(8,128)(2,1)} copy(bf16[1,1,160,512]{3,2,1,0:T(8,128)(2,1)S(1)} %shard_map.136) | data formatting | bytes 327680

commit v2 on v1

--- a/solution.py
+++ b/solution.py
@@ -12,9 +12,8 @@
 BLOCK = 8
 LANES = 128
 DIGIT = 256
-CHUNK = 512
-SIDES_AT = 0
-CORNERS_AT = 1
+CHUNK = 256
+UP_AT = 1
 MESH = pl.DeviceIdType.MESH
 
 BF16 = jnp.bfloat16
@@ -80,11 +79,15 @@
     nbias_v,
     table,
     edge_table,
-    picks_e,
-    picks_n,
+    low_v,
+    high_v,
+    spot_v,
+    tail_v,
     before,
     put_sum,
     got_sum,
+    w_center,
+    node_v,
     load_sem,
     send_sem,
     recv_sem,
@@ -112,22 +115,39 @@
         else:
             pl.when(lat > 0 if dlat < 0 else lat < n_lat - 1)(body)
 
+    edge_table[...] = jnp.zeros(edge_table.shape, BF16)
+    got_sum[...] = jnp.zeros(got_sum.shape, BF16)
+
+    barrier = pltpu.get_barrier_semaphore()
+
+    def greet(dlat, dlon):
+        pl.semaphore_signal(barrier, inc=1, device_id=there(dlat, dlon), device_id_type=MESH)
+
+    greet(0, -1)
+    greet(0, 1)
+    guarded(-1, lambda: greet(-1, 0))
+    guarded(1, lambda: greet(1, 0))
+
     groups = [
         [(snd_h.at[0], snd_v)],
-        [(w_grid_h, w_grid_v), (grid_h.at[0, 0], grid_v)],
         [
             (mesh_h.at[0, 0], mesh_v),
             (w_mesh_h, w_mesh_v),
+            (w_edge_h, w_edge_v),
             (rcv_h.at[0], rcv_v),
             (geo_h.at[0, 0], geo_v),
-            (w_edge_h, w_edge_v),
         ],
         [(bias_h, bias_v), (gain_h, gain_v), (nbias_h, nbias_v)],
+        [(w_grid_h, w_grid_v), (grid_h.at[0, 0], grid_v)],
         [(w_message_h, w_message_v), (w_node_h, w_node_v), (w_output_h, w_output_v)],
     ]
-    for number, group in enumerate(groups):
-        for source, target in group:
+
+    def load(number):
+        for source, target in groups[number]:
             pltpu.make_async_copy(source, target, load_sem.at[number]).start()
+
+    for number in range(4):
+        load(number)
 
     def bytes_of(ref):
         return ref.dtype.itemsize * functools.reduce(lambda a, b: a * b, ref.shape)
@@ -142,19 +162,6 @@
     def loaded(number):
         view = span_of(sum(bytes_of(target) for _, target in groups[number]))
         pltpu.make_async_copy(view, view, load_sem.at[number]).wait()
-
-    edge_table[...] = jnp.zeros(edge_table.shape, BF16)
-    got_sum[...] = jnp.zeros(got_sum.shape, BF16)
-
-    barrier = pltpu.get_barrier_semaphore()
-
-    def greet(dlat, dlon):
-        pl.semaphore_signal(barrier, inc=1, device_id=there(dlat, dlon), device_id_type=MESH)
-
-    greet(0, -1)
-    greet(0, 1)
-    guarded(-1, lambda: greet(-1, 0))
-    guarded(1, lambda: greet(1, 0))
 
     def offset(slot):
         return slot // 3 - 1, slot % 3 - 1
@@ -184,22 +191,23 @@
         size = size_of(slot)
         return pltpu.make_async_remote_copy(
             src_ref=put_sum.at[pl.ds(place(slot) - rows, size)],
-            dst_ref=got_sum.at[pl.ds(strip(slot) * B_SIDE, size)],
-            send_sem=send_sem.at[4 + dlat],
+            dst_ref=got_sum.at[pl.ds(place(slot) - rows, size)],
+            send_sem=send_sem.at[1 + dlat],
             recv_sem=recv_sem.at[4 - dlat],
             device_id=there(dlat, dlon),
             device_id_type=MESH,
         )
 
-    def settle(sems, first):
+    def settle(sems, first, chosen, times=1):
         for dlat in (-1, 1, 0):
-
-            def body(dlat=dlat):
-                count = sum(size_of(s) for s in SIDES + CORNERS if offset(s)[0] == dlat)
-                view = table.at[pl.ds(0, count)]
-                pltpu.make_async_copy(view, view, sems.at[first + 1 + dlat]).wait()
-
-            guarded(dlat, body)
+            count = times * sum(size_of(s) for s in chosen if offset(s)[0] == dlat)
+            if count:
+
+                def body(dlat=dlat, count=count):
+                    view = table.at[pl.ds(0, count)]
+                    pltpu.make_async_copy(view, view, sems.at[first + 1 + dlat]).wait()
+
+                guarded(dlat, body)
 
     def each(chosen, sign, action):
         for dlat in (-1, 1, 0):
@@ -215,7 +223,6 @@
     def send_sides():
         arrivals = 2 + (lat > 0).astype(jnp.int32) + (lat < n_lat - 1).astype(jnp.int32)
         pl.semaphore_wait(barrier, arrivals)
-        each(SIDES, -1, lambda s: mesh_copy(s).start())
         for dlat in (-1, 1):
 
             def tell(dlat=dlat):
@@ -227,17 +234,16 @@
                 )
 
             guarded(dlat, tell)
-
-    def send_corners():
-        for dlat in (-1, 1):
-
-            def go(dlat=dlat):
-                pl.semaphore_wait(ready_sem.at[0 if dlat < 0 else 1], 1)
-                for s in CORNERS:
-                    if offset(s)[0] == -dlat:
-                        mesh_copy(s).start()
-
-            guarded(dlat, go)
+        each(SIDES, -1, lambda s: mesh_copy(s).start())
+
+    def send_corners(dlat):
+        def go():
+            pl.semaphore_wait(ready_sem.at[0 if dlat < 0 else 1], 1)
+            for s in CORNERS:
+                if offset(s)[0] == -dlat:
+                    mesh_copy(s).start()
+
+        guarded(dlat, go)
 
     step = min(CHUNK, edges)
     starts = list(range(0, edges, step))
@@ -250,19 +256,14 @@
     upper = lax.shift_left(lax.shift_right_logical(senders, 8), 8)
     lower = (senders - upper).astype(F32).astype(BF16)
     upper = upper.astype(F32).astype(BF16)
-    loaded(1)
-    table[:grid_rows, :] = (0.5 * nn(grid_v[...], w_grid_v[...])).astype(BF16)
+
     for start in starts:
         span = pl.ds(start, step)
-        low = down(lower[:, start : start + step], LANES)
-        high = down(upper[:, start : start + step], LANES)
-        for q in range(digits):
-            digit = (high - float(DIGIT * q)) + low
-            for h in range(DIGIT // LANES):
-                picks_e[span, pl.ds(q * DIGIT + h * LANES, LANES)] = equal(digit, lanes[h])
-
+        low_v[span, :] = down(lower[:, start : start + step], LANES)
+        high_v[span, :] = down(upper[:, start : start + step], LANES)
+
+    loaded(1)
     loaded(2)
-    loaded(3)
     high, low = [part.astype(F32) for part in halves(w_edge_v[...])]
     bias_high, bias_low = [part.astype(F32) for part in halves(bias_v[...])]
     blank = jnp.zeros((BLOCK - B_CORNER, features), F32)
@@ -278,7 +279,7 @@
             0,
         )
     ).astype(BF16)
-
+    send_sides()
     picks = rcv_v[...]
     shift, spot = 0, picks
     for s in range(9):
@@ -299,58 +300,82 @@
     ).astype(BF16)
     for start in starts:
         span = pl.ds(start, step)
-        at = down(spot[:, start : start + step], LANES)
-        for h in range(slots // LANES):
-            found = equal(at, lanes[h])
-            if h * LANES == cut:
-                found = found + jnp.transpose(tail[:, start : start + step])
-            picks_e[span, pl.ds(grid_rows + h * LANES, LANES)] = found
-    row = lax.broadcasted_iota(jnp.int32, (slots, step), 0).astype(F32).astype(BF16)
-    for start in starts:
-        at = jnp.broadcast_to(spot[:, start : start + step], (slots, step))
-        picks_n[:, pl.ds(start, step)] = equal(row, at)
+        spot_v[span, :] = down(spot[:, start : start + step], LANES)
+        tail_v[span, :] = jnp.transpose(tail[:, start : start + step])
+
+    send_corners(-1)
+    loaded(3)
+    load(4)
+    table[:grid_rows, :] = (0.5 * nn(grid_v[...], w_grid_v[...])).astype(BF16)
+
+    def picked(span, first):
+        tiles = []
+        for h in range(first, slots // LANES):
+            found = equal(spot_v[span, :], lanes[h])
+            tiles.append(found + tail_v[span, :] if h * LANES == cut else found)
+        return tiles
 
     for number, start in enumerate(starts):
-        if number == SIDES_AT:
-            send_sides()
-        if number == CORNERS_AT:
-            send_corners()
+        if number == UP_AT:
+            send_corners(1)
         span = pl.ds(start, step)
-        before[span, :] = nn(picks_e[span, :], table[...])
-
-    settle(recv_sem, 0)
-
-    summed = None
+        tiles = []
+        for q in range(digits):
+            digit = (high_v[span, :] - float(DIGIT * q)) + low_v[span, :]
+            tiles += [equal(digit, lanes[h]) for h in range(DIGIT // LANES)]
+        before[span, :] = nn(jnp.concatenate(tiles + picked(span, 0), 1), table[...])
+
+    settle(recv_sem, 0, SIDES + CORNERS)
+
+    parts = []
     for start in starts:
         span = pl.ds(start, step)
-        half = before[span, :] + nn(picks_e[span, grid_rows + cut :], edge_table[...])
-        hidden = (half + half * jnp.tanh(half)).astype(BF16)
-        added = nn(picks_n[:, span], hidden)
-        summed = added if summed is None else summed + added
+        tiles = picked(span, cut // LANES)
+        half = before[span, :] + nn(jnp.concatenate(tiles, 1), edge_table[...])
+        parts.append((half + half * jnp.tanh(half)).astype(BF16))
+    row = lax.broadcasted_iota(jnp.int32, (slots, edges), 0).astype(F32).astype(BF16)
+    at = jnp.broadcast_to(spot, (slots, edges))
+    summed = nn(equal(row, at), jnp.concatenate(parts, 0))
 
     put_sum[...] = summed[rows:, :].astype(BF16)
-    each(SIDES + CORNERS, 1, lambda s: sum_copy(s).start())
+    each(CORNERS, 1, lambda s: sum_copy(s).start())
+    each(SIDES, 1, lambda s: sum_copy(s).start())
 
     loaded(4)
     fold = nn(w_message_v[...], w_node_v[features:, :]).astype(BF16)
     high, low = halves(summed[:rows, :])
-    node = nn(mesh_v[...], w_node_v[:features, :]) + nn(high, fold) + nn(low, fold)
-
-    def finish(node, span):
+    node_v[...] = (
+        nn(mesh_v[...], w_node_v[:features, :]) + nn(high, fold) + nn(low, fold)
+    )
+    weights = w_output_v[...].astype(F32)
+    center = jnp.mean(weights, axis=-1, keepdims=True)
+    w_center[...] = (weights - center).astype(BF16)
+
+    def rows_of(ref, spans):
+        return jnp.concatenate([ref[pl.ds(*span), :].astype(F32) for span in spans], 0)
+
+    def finish(spans, extra=None):
+        node = rows_of(node_v, spans)
+        if extra is not None:
+            node = node + nn(extra[...], fold)
         node_hidden = (node * jax.nn.sigmoid(node)).astype(BF16)
-        update = nn(node_hidden, w_output_v[...])
-        row_mean = jnp.mean(update, axis=-1, keepdims=True)
-        centered = update - row_mean
+        centered = nn(node_hidden, w_center[...])
         row_var = jnp.mean(centered * centered, axis=-1, keepdims=True)
         normed = centered * lax.rsqrt(row_var + 1e-05) * gain_v[...] + nbias_v[...]
-        out_ref[0, 0, span, :] = (mesh_v[span, :].astype(F32) + normed).astype(BF16)
-
-    finish(node[border:], pl.ds(border, rows - border))
-    settle(recv_sem, 3)
-    finish(node[:border] + nn(got_sum[...], fold), pl.ds(0, border))
-
-    settle(send_sem, 0)
-    settle(send_sem, 3)
+        result = rows_of(mesh_v, spans) + normed
+        first = 0
+        for start, count in spans:
+            out_ref[0, 0, pl.ds(start, count), :] = result[first : first + count].astype(BF16)
+            first += count
+
+    at_sides = [(strip(s) * B_SIDE, B_SIDE) for s in SIDES]
+    at_corners = [(strip(s) * B_SIDE, BLOCK) for s in CORNERS]
+    between = [(strip(s) * B_SIDE + BLOCK, B_SIDE - BLOCK) for s in CORNERS]
+    finish([(border, rows - border)] + between)
+    settle(recv_sem, 3, SIDES + CORNERS)
+    finish(at_sides + at_corners, got_sum)
+
+    settle(send_sem, 0, SIDES + CORNERS, 2)
 
 
 def local(n_lon, n_lat, *args):
@@ -374,13 +399,17 @@
         + [
             pltpu.VMEM((grid_rows + slots, features), BF16),
             pltpu.VMEM((slots - cut, features), BF16),
-            pltpu.VMEM((edges, grid_rows + slots), BF16),
-            pltpu.VMEM((slots, edges), BF16),
+            pltpu.VMEM((edges, LANES), BF16),
+            pltpu.VMEM((edges, LANES), BF16),
+            pltpu.VMEM((edges, LANES), BF16),
+            pltpu.VMEM((edges, LANES), BF16),
             pltpu.VMEM((edges, features), F32),
             pltpu.VMEM((slots - rows, features), BF16),
-            pltpu.VMEM((8 * B_SIDE, features), BF16),
+            pltpu.VMEM((slots - rows, features), BF16),
+            pltpu.VMEM((features, features), BF16),
+            pltpu.VMEM((rows, features), F32),
             pltpu.SemaphoreType.DMA((5,)),
-            pltpu.SemaphoreType.DMA((6,)),
+            pltpu.SemaphoreType.DMA((3,)),
             pltpu.SemaphoreType.DMA((6,)),
             pltpu.SemaphoreType.REGULAR((2,)),
         ],

time: 16.2 us -> 14.2 us (0.88)
  Pallas kernels: 15.4 us -> 13.3 us
    pallas_call x1, Pallas kernels: 15.4 us -> 13.3 us  [local(): pl.pallas_call(functools.partial(kernel, n_lon, n_lat), out_shape=pltpu.V...]
where the time goes in v2:
time: 14.2 us; the launch traced here: 14 us
  Pallas kernels  13.3 us (94%)
  local copies, waits for them, and re-layouts  0.67 us (5%)
    pallas_call x1, Pallas kernels, local(): pl.pallas_call(functools.partial(kernel, n_lon, n_lat), out_shape=pltpu.V...  13.3 us
    unnamed x1, local copies, waits for them, and re-layouts  0.67 us

profile of v2, /device:TPU:0, one launch (start us, length us, event | category | flops | bytes accessed | tf_op | source)
XLA Modules:
  0.0 14.0 jit_solution(5295406292867503123)
XLA Ops:
  0.0 13.3 %shard_map.136 = bf16[1,1,160,512]{3,2,1,0:T(8,128)(2,1)S(1)} custom-call(bf16[1,1,1024,512]{3,2,1,0:T(8,128)(2,1)} %grid_h.1, bf16[1,1,160,512]{3,2,1,0:T(8,128)(2,1)} %mesh_h.1, f32[1,1,4,2048]{3,2,1,0:T(4,128)} %geo_h.1, s32[1,1,2048]{2,1,0:T(1,128)} %snd_h.1, s32[1,1,2048]{2,1,0:T(1,128)} %rcv_h.1, bf16[512,512]{1,0:T(8,128)(2,1)} %w_grid_h.1, ...), custom_call_target="tpu_custom_call" | custom-call | tf_op jit(solution)/shard_map/pallas_call | solution.py:393
  13.3 0.7 %copy.16 = bf16[1,1,160,512]{3,2,1,0:T(8,128)(2,1)} copy(bf16[1,1,160,512]{3,2,1,0:T(8,128)(2,1)S(1)} %shard_map.136) | data formatting | bytes 327680

commit v3 on v2

--- a/solution.py
+++ b/solution.py
@@ -18,9 +18,11 @@
 
 BF16 = jnp.bfloat16
 F32 = jnp.float32
+F8 = jnp.float8_e4m3fn
 
 SIDES = (1, 3, 5, 7)
 CORNERS = (0, 2, 6, 8)
+SENT = (2, 1, 0, 3, 5, 7, 8, 6)
 
 
 def strip(slot):
@@ -81,8 +83,7 @@
     edge_table,
     low_v,
     high_v,
-    spot_v,
-    tail_v,
+    picks_8,
     before,
     put_sum,
     got_sum,
@@ -210,7 +211,7 @@
                 guarded(dlat, body)
 
     def each(chosen, sign, action):
-        for dlat in (-1, 1, 0):
+        for dlat in (-1, 0, 1):
             members = [s for s in chosen if offset(s)[0] == sign * dlat]
             if members:
 
@@ -280,6 +281,11 @@
         )
     ).astype(BF16)
     send_sides()
+    send_corners(-1)
+    loaded(3)
+    load(4)
+    table[:grid_rows, :] = (0.5 * nn(grid_v[...], w_grid_v[...])).astype(BF16)
+
     picks = rcv_v[...]
     shift, spot = 0, picks
     for s in range(9):
@@ -298,52 +304,49 @@
         + [empty, high, empty, high, empty, low, empty, ones],
         0,
     ).astype(BF16)
-    for start in starts:
-        span = pl.ds(start, step)
-        spot_v[span, :] = down(spot[:, start : start + step], LANES)
-        tail_v[span, :] = jnp.transpose(tail[:, start : start + step])
-
-    send_corners(-1)
-    loaded(3)
-    load(4)
-    table[:grid_rows, :] = (0.5 * nn(grid_v[...], w_grid_v[...])).astype(BF16)
-
-    def picked(span, first):
-        tiles = []
-        for h in range(first, slots // LANES):
-            found = equal(spot_v[span, :], lanes[h])
-            tiles.append(found + tail_v[span, :] if h * LANES == cut else found)
-        return tiles
-
     for number, start in enumerate(starts):
         if number == UP_AT:
             send_corners(1)
         span = pl.ds(start, step)
+        at = down(spot[:, start : start + step], LANES)
         tiles = []
         for q in range(digits):
             digit = (high_v[span, :] - float(DIGIT * q)) + low_v[span, :]
             tiles += [equal(digit, lanes[h]) for h in range(DIGIT // LANES)]
-        before[span, :] = nn(jnp.concatenate(tiles + picked(span, 0), 1), table[...])
+        for h in range(slots // LANES):
+            found = equal(at, lanes[h])
+            if h * LANES == cut:
+                twice = found.astype(F8)
+                picks_8[span, :] = jnp.concatenate([twice, twice], 1)
+                found = found + jnp.transpose(tail[:, start : start + step])
+            tiles.append(found)
+        before[span, :] = nn(jnp.concatenate(tiles, 1), table[...])
 
     settle(recv_sem, 0, SIDES + CORNERS)
 
+    arrived = edge_table[...].astype(F32)
+    rough = arrived.astype(F8)
+    fine = (arrived - rough.astype(F32)).astype(F8)
+    split = jnp.concatenate([rough, fine], 0)
     parts = []
     for start in starts:
         span = pl.ds(start, step)
-        tiles = picked(span, cut // LANES)
-        half = before[span, :] + nn(jnp.concatenate(tiles, 1), edge_table[...])
-        parts.append((half + half * jnp.tanh(half)).astype(BF16))
-    row = lax.broadcasted_iota(jnp.int32, (slots, edges), 0).astype(F32).astype(BF16)
-    at = jnp.broadcast_to(spot, (slots, edges))
-    summed = nn(equal(row, at), jnp.concatenate(parts, 0))
-
-    put_sum[...] = summed[rows:, :].astype(BF16)
-    each(CORNERS, 1, lambda s: sum_copy(s).start())
-    each(SIDES, 1, lambda s: sum_copy(s).start())
+        half = before[span, :] + nn(picks_8[span, :], split)
+        half = half.astype(BF16)
+        parts.append(half + half * jnp.tanh(half))
+    hidden = jnp.concatenate(parts, 0)
+
+    def gathered(first, count):
+        row = lax.broadcasted_iota(jnp.int32, (count, edges), 0) + first
+        at = jnp.broadcast_to(spot, (count, edges))
+        return nn(equal(row.astype(F32).astype(BF16), at), hidden)
+
+    put_sum[...] = gathered(rows, slots - rows).astype(BF16)
+    each(SENT, 1, lambda s: sum_copy(s).start())
 
     loaded(4)
     fold = nn(w_message_v[...], w_node_v[features:, :]).astype(BF16)
-    high, low = halves(summed[:rows, :])
+    high, low = halves(gathered(0, rows))
     node_v[...] = (
         nn(mesh_v[...], w_node_v[:features, :]) + nn(high, fold) + nn(low, fold)
     )
@@ -401,8 +404,7 @@
             pltpu.VMEM((slots - cut, features), BF16),
             pltpu.VMEM((edges, LANES), BF16),
             pltpu.VMEM((edges, LANES), BF16),
-            pltpu.VMEM((edges, LANES), BF16),
-            pltpu.VMEM((edges, LANES), BF16),
+            pltpu.VMEM((edges, 2 * LANES), F8),
             pltpu.VMEM((edges, features), F32),
             pltpu.VMEM((slots - rows, features), BF16),
             pltpu.VMEM((slots - rows, features), BF16),

time: 14.2 us -> 13.8 us (0.972)
  Pallas kernels: 13.3 us -> 12.9 us
    pallas_call x1, Pallas kernels: 13.3 us -> 12.9 us  [local(): pl.pallas_call(functools.partial(kernel, n_lon, n_lat), out_shape=pltpu.V...]
where the time goes in v3:
time: 13.8 us; the launch traced here: 13.6 us
  Pallas kernels  12.9 us (93%)
  local copies, waits for them, and re-layouts  0.67 us (5%)
    pallas_call x1, Pallas kernels, local(): pl.pallas_call(functools.partial(kernel, n_lon, n_lat), out_shape=pltpu.V...  12.9 us
    unnamed x1, local copies, waits for them, and re-layouts  0.67 us

profile of v3, /device:TPU:0, one launch (start us, length us, event | category | flops | bytes accessed | tf_op | source)
XLA Modules:
  0.0 13.6 jit_solution(10598451065936166700)
XLA Ops:
  0.0 12.9 %shard_map.136 = bf16[1,1,160,512]{3,2,1,0:T(8,128)(2,1)S(1)} custom-call(bf16[1,1,1024,512]{3,2,1,0:T(8,128)(2,1)} %grid_h.1, bf16[1,1,160,512]{3,2,1,0:T(8,128)(2,1)} %mesh_h.1, f32[1,1,4,2048]{3,2,1,0:T(4,128)} %geo_h.1, s32[1,1,2048]{2,1,0:T(1,128)} %snd_h.1, s32[1,1,2048]{2,1,0:T(1,128)} %rcv_h.1, bf16[512,512]{1,0:T(8,128)(2,1)} %w_grid_h.1, ...), custom_call_target="tpu_custom_call" | custom-call | tf_op jit(solution)/shard_map/pallas_call | solution.py:396
  12.9 0.7 %copy.16 = bf16[1,1,160,512]{3,2,1,0:T(8,128)(2,1)} copy(bf16[1,1,160,512]{3,2,1,0:T(8,128)(2,1)S(1)} %shard_map.136) | data formatting | bytes 327680

commit v4 on v3

--- a/solution.py
+++ b/solution.py
@@ -14,6 +14,8 @@
 DIGIT = 256
 CHUNK = 256
 UP_AT = 1
+BURSTS = (1, 2, 3, 2)
+LAG = 1
 MESH = pl.DeviceIdType.MESH
 
 BF16 = jnp.bfloat16
@@ -240,7 +242,7 @@
     def send_corners(dlat):
         def go():
             pl.semaphore_wait(ready_sem.at[0 if dlat < 0 else 1], 1)
-            for s in CORNERS:
+            for s in reversed(CORNERS):
                 if offset(s)[0] == -dlat:
                     mesh_copy(s).start()
 
@@ -328,25 +330,35 @@
     rough = arrived.astype(F8)
     fine = (arrived - rough.astype(F32)).astype(F8)
     split = jnp.concatenate([rough, fine], 0)
-    parts = []
-    for start in starts:
-        span = pl.ds(start, step)
-        half = before[span, :] + nn(picks_8[span, :], split)
-        half = half.astype(BF16)
-        parts.append(half + half * jnp.tanh(half))
-    hidden = jnp.concatenate(parts, 0)
-
-    def gathered(first, count):
-        row = lax.broadcasted_iota(jnp.int32, (count, edges), 0) + first
-        at = jnp.broadcast_to(spot, (count, edges))
+    def gathered(first, count, begin, hidden):
+        width = hidden.shape[0]
+        row = lax.broadcasted_iota(jnp.int32, (count, width), 0) + first
+        at = jnp.broadcast_to(spot[:, begin : begin + width], (count, width))
         return nn(equal(row.astype(F32).astype(BF16), at), hidden)
 
-    put_sum[...] = gathered(rows, slots - rows).astype(BF16)
+    unit = edges // sum(BURSTS)
+    sizes = [unit * count for count in BURSTS]
+    begins = [sum(sizes[:number]) for number in range(len(sizes))]
+    halves_of, parts, summed = [], [], None
+    for number in range(len(sizes) + LAG):
+        if number < len(sizes):
+            span = pl.ds(begins[number], sizes[number])
+            half = before[span, :] + nn(picks_8[span, :], split)
+            halves_of.append(half.astype(BF16))
+        if 1 <= number <= len(sizes):
+            half = halves_of[number - 1]
+            parts.append(half + half * jnp.tanh(half))
+        if number >= LAG:
+            done = number - LAG
+            added = gathered(rows, slots - rows, begins[done], parts[done])
+            summed = added if summed is None else summed + added
+
+    put_sum[...] = summed.astype(BF16)
     each(SENT, 1, lambda s: sum_copy(s).start())
 
     loaded(4)
     fold = nn(w_message_v[...], w_node_v[features:, :]).astype(BF16)
-    high, low = halves(gathered(0, rows))
+    high, low = halves(gathered(0, rows, 0, jnp.concatenate(parts, 0)))
     node_v[...] = (
         nn(mesh_v[...], w_node_v[:features, :]) + nn(high, fold) + nn(low, fold)
     )

time: 13.8 us -> 13.7 us (level)
  no operation moved by 1% of the time
where the time goes in v4:
time: 13.7 us; the launch traced here: 13.5 us
  Pallas kernels  12.8 us (93%)
  local copies, waits for them, and re-layouts  0.67 us (5%)
    pallas_call x1, Pallas kernels, local(): pl.pallas_call(functools.partial(kernel, n_lon, n_lat), out_shape=pltpu.V...  12.8 us
    unnamed x1, local copies, waits for them, and re-layouts  0.67 us

profile of v4, /device:TPU:0, one launch (start us, length us, event | category | flops | bytes accessed | tf_op | source)
XLA Modules:
  0.0 13.5 jit_solution(15841134299541596772)
XLA Ops:
  0.0 12.8 %shard_map.136 = bf16[1,1,160,512]{3,2,1,0:T(8,128)(2,1)S(1)} custom-call(bf16[1,1,1024,512]{3,2,1,0:T(8,128)(2,1)} %grid_h.1, bf16[1,1,160,512]{3,2,1,0:T(8,128)(2,1)} %mesh_h.1, f32[1,1,4,2048]{3,2,1,0:T(4,128)} %geo_h.1, s32[1,1,2048]{2,1,0:T(1,128)} %snd_h.1, s32[1,1,2048]{2,1,0:T(1,128)} %rcv_h.1, bf16[512,512]{1,0:T(8,128)(2,1)} %w_grid_h.1, ...), custom_call_target="tpu_custom_call" | custom-call | tf_op jit(solution)/shard_map/pallas_call | solution.py:408
  12.8 0.7 %copy.16 = bf16[1,1,160,512]{3,2,1,0:T(8,128)(2,1)} copy(bf16[1,1,160,512]{3,2,1,0:T(8,128)(2,1)S(1)} %shard_map.136) | data formatting | bytes 327680

commit v5 on v4

--- a/solution.py
+++ b/solution.py
@@ -91,9 +91,9 @@
     got_sum,
     w_center,
     node_v,
+    ruler,
     load_sem,
-    send_sem,
-    recv_sem,
+    strip_sem,
     ready_sem,
 ):
     lon = lax.axis_index("lon")
@@ -139,32 +139,31 @@
             (w_edge_h, w_edge_v),
             (rcv_h.at[0], rcv_v),
             (geo_h.at[0, 0], geo_v),
+            (bias_h, bias_v),
+            (gain_h, gain_v),
+            (nbias_h, nbias_v),
         ],
-        [(bias_h, bias_v), (gain_h, gain_v), (nbias_h, nbias_v)],
         [(w_grid_h, w_grid_v), (grid_h.at[0, 0], grid_v)],
         [(w_message_h, w_message_v), (w_node_h, w_node_v), (w_output_h, w_output_v)],
     ]
 
     def load(number):
         for source, target in groups[number]:
-            pltpu.make_async_copy(source, target, load_sem.at[number]).start()
-
-    for number in range(4):
+            pltpu.make_async_copy(source, target, load_sem.at[number % 3]).start()
+
+    for number in range(3):
         load(number)
 
     def bytes_of(ref):
         return ref.dtype.itemsize * functools.reduce(lambda a, b: a * b, ref.shape)
 
-    def span_of(total):
-        if total < bytes_of(snd_v):
-            return snd_v.at[:, pl.ds(0, total // snd_v.dtype.itemsize)]
-        if total < bytes_of(table):
-            return table.at[pl.ds(0, total // (2 * features))]
-        return before.at[pl.ds(0, total // (4 * features))]
+    def await_bytes(total, sem):
+        view = ruler.at[:, pl.ds(0, total // ruler.dtype.itemsize)]
+        pltpu.make_async_copy(view, view, sem).wait()
 
     def loaded(number):
-        view = span_of(sum(bytes_of(target) for _, target in groups[number]))
-        pltpu.make_async_copy(view, view, load_sem.at[number]).wait()
+        total = sum(bytes_of(target) for _, target in groups[number])
+        await_bytes(total, load_sem.at[number % 3])
 
     def offset(slot):
         return slot // 3 - 1, slot % 3 - 1
@@ -183,8 +182,8 @@
         return pltpu.make_async_remote_copy(
             src_ref=table.at[pl.ds(grid_rows + strip(slot) * B_SIDE, size)],
             dst_ref=edge_table.at[pl.ds(place(slot) - cut, size)],
-            send_sem=send_sem.at[1 - dlat],
-            recv_sem=recv_sem.at[1 + dlat],
+            send_sem=strip_sem.at[0],
+            recv_sem=strip_sem.at[1],
             device_id=there(-dlat, -dlon),
             device_id_type=MESH,
         )
@@ -195,22 +194,22 @@
         return pltpu.make_async_remote_copy(
             src_ref=put_sum.at[pl.ds(place(slot) - rows, size)],
             dst_ref=got_sum.at[pl.ds(place(slot) - rows, size)],
-            send_sem=send_sem.at[1 + dlat],
-            recv_sem=recv_sem.at[4 - dlat],
+            send_sem=strip_sem.at[0],
+            recv_sem=strip_sem.at[2],
             device_id=there(dlat, dlon),
             device_id_type=MESH,
         )
 
-    def settle(sems, first, chosen, times=1):
-        for dlat in (-1, 1, 0):
-            count = times * sum(size_of(s) for s in chosen if offset(s)[0] == dlat)
-            if count:
-
-                def body(dlat=dlat, count=count):
-                    view = table.at[pl.ds(0, count)]
-                    pltpu.make_async_copy(view, view, sems.at[first + 1 + dlat]).wait()
-
-                guarded(dlat, body)
+    bands = (lat > 0).astype(jnp.int32) + (lat < n_lat - 1).astype(jnp.int32)
+
+    def settle(sem, times):
+        for count in range(3):
+
+            def body(count=count):
+                lines = 2 * B_SIDE + count * (B_SIDE + 2 * B_CORNER)
+                await_bytes(times * lines * features * 2, sem)
+
+            pl.when(bands == count)(body)
 
     def each(chosen, sign, action):
         for dlat in (-1, 0, 1):
@@ -224,8 +223,7 @@
                 guarded(dlat, body)
 
     def send_sides():
-        arrivals = 2 + (lat > 0).astype(jnp.int32) + (lat < n_lat - 1).astype(jnp.int32)
-        pl.semaphore_wait(barrier, arrivals)
+        pl.semaphore_wait(barrier, 2 + bands)
         for dlat in (-1, 1):
 
             def tell(dlat=dlat):
@@ -266,7 +264,6 @@
         high_v[span, :] = down(upper[:, start : start + step], LANES)
 
     loaded(1)
-    loaded(2)
     high, low = [part.astype(F32) for part in halves(w_edge_v[...])]
     bias_high, bias_low = [part.astype(F32) for part in halves(bias_v[...])]
     blank = jnp.zeros((BLOCK - B_CORNER, features), F32)
@@ -284,8 +281,8 @@
     ).astype(BF16)
     send_sides()
     send_corners(-1)
-    loaded(3)
-    load(4)
+    loaded(2)
+    load(3)
     table[:grid_rows, :] = (0.5 * nn(grid_v[...], w_grid_v[...])).astype(BF16)
 
     picks = rcv_v[...]
@@ -324,7 +321,7 @@
             tiles.append(found)
         before[span, :] = nn(jnp.concatenate(tiles, 1), table[...])
 
-    settle(recv_sem, 0, SIDES + CORNERS)
+    settle(strip_sem.at[1], 1)
 
     arrived = edge_table[...].astype(F32)
     rough = arrived.astype(F8)
@@ -356,7 +353,7 @@
     put_sum[...] = summed.astype(BF16)
     each(SENT, 1, lambda s: sum_copy(s).start())
 
-    loaded(4)
+    loaded(3)
     fold = nn(w_message_v[...], w_node_v[features:, :]).astype(BF16)
     high, low = halves(gathered(0, rows, 0, jnp.concatenate(parts, 0)))
     node_v[...] = (
@@ -387,10 +384,10 @@
     at_corners = [(strip(s) * B_SIDE, BLOCK) for s in CORNERS]
     between = [(strip(s) * B_SIDE + BLOCK, B_SIDE - BLOCK) for s in CORNERS]
     finish([(border, rows - border)] + between)
-    settle(recv_sem, 3, SIDES + CORNERS)
+    settle(strip_sem.at[2], 1)
     finish(at_sides + at_corners, got_sum)
 
-    settle(send_sem, 0, SIDES + CORNERS, 2)
+    settle(strip_sem.at[0], 2)
 
 
 def local(n_lon, n_lat, *args):
@@ -401,6 +398,7 @@
     edges = senders.shape[2]
     slots = rows + 4 * B_SIDE + 4 * BLOCK
     cut = rows // LANES * LANES
+    ruler = sum(a.size * a.dtype.itemsize for a in args[9:12]) // 4
     loads = []
     for number, a in enumerate(args):
         shape = a.shape[2:] if number < 3 else a.shape[1:] if number < 5 else a.shape
@@ -422,9 +420,9 @@
             pltpu.VMEM((slots - rows, features), BF16),
             pltpu.VMEM((features, features), BF16),
             pltpu.VMEM((rows, features), F32),
-            pltpu.SemaphoreType.DMA((5,)),
+            pltpu.VMEM((1, ruler), jnp.int32),
             pltpu.SemaphoreType.DMA((3,)),
-            pltpu.SemaphoreType.DMA((6,)),
+            pltpu.SemaphoreType.DMA((3,)),
             pltpu.SemaphoreType.REGULAR((2,)),
         ],
         compiler_params=pltpu.CompilerParams(

time: 13.7 us -> 13.6 us (level)
  no operation moved by 1% of the time
where the time goes in v5:
time: 13.6 us; the launch traced here: 13.4 us
  Pallas kernels  12.7 us (93%)
  local copies, waits for them, and re-layouts  0.67 us (5%)
    pallas_call x1, Pallas kernels, local(): pl.pallas_call(functools.partial(kernel, n_lon, n_lat), out_shape=pltpu.V...  12.7 us
    unnamed x1, local copies, waits for them, and re-layouts  0.67 us

profile of v5, /device:TPU:0, one launch (start us, length us, event | category | flops | bytes accessed | tf_op | source)
XLA Modules:
  0.0 13.4 jit_solution(16816321759306882921)
XLA Ops:
  0.0 12.7 %shard_map.136 = bf16[1,1,160,512]{3,2,1,0:T(8,128)(2,1)S(1)} custom-call(bf16[1,1,1024,512]{3,2,1,0:T(8,128)(2,1)} %grid_h.1, bf16[1,1,160,512]{3,2,1,0:T(8,128)(2,1)} %mesh_h.1, f32[1,1,4,2048]{3,2,1,0:T(4,128)} %geo_h.1, s32[1,1,2048]{2,1,0:T(1,128)} %snd_h.1, s32[1,1,2048]{2,1,0:T(1,128)} %rcv_h.1, bf16[512,512]{1,0:T(8,128)(2,1)} %w_grid_h.1, ...), custom_call_target="tpu_custom_call" | custom-call | tf_op jit(solution)/shard_map/pallas_call | solution.py:406
  12.7 0.7 %copy.16 = bf16[1,1,160,512]{3,2,1,0:T(8,128)(2,1)} copy(bf16[1,1,160,512]{3,2,1,0:T(8,128)(2,1)S(1)} %shard_map.136) | data formatting | bytes 327680

commit v6 on v5

--- a/solution.py
+++ b/solution.py
@@ -14,7 +14,7 @@
 DIGIT = 256
 CHUNK = 256
 UP_AT = 1
-BURSTS = (1, 2, 3, 2)
+BURSTS = (1, 1, 2, 2, 2)
 LAG = 1
 MESH = pl.DeviceIdType.MESH
 
@@ -341,10 +341,10 @@
         if number < len(sizes):
             span = pl.ds(begins[number], sizes[number])
             half = before[span, :] + nn(picks_8[span, :], split)
-            halves_of.append(half.astype(BF16))
+            halves_of.append(half)
         if 1 <= number <= len(sizes):
             half = halves_of[number - 1]
-            parts.append(half + half * jnp.tanh(half))
+            parts.append((half + half * jnp.tanh(half)).astype(BF16))
         if number >= LAG:
             done = number - LAG
             added = gathered(rows, slots - rows, begins[done], parts[done])

time: 13.6 us -> 13.7 us (level)
  no operation moved by 1% of the time
where the time goes in v6:
time: 13.7 us; the launch traced here: 13.5 us
  Pallas kernels  12.8 us (93%)
  local copies, waits for them, and re-layouts  0.67 us (5%)
    pallas_call x1, Pallas kernels, local(): pl.pallas_call(functools.partial(kernel, n_lon, n_lat), out_shape=pltpu.V...  12.8 us
    unnamed x1, local copies, waits for them, and re-layouts  0.67 us

profile of v6, /device:TPU:0, one launch (start us, length us, event | category | flops | bytes accessed | tf_op | source)
XLA Modules:
  0.0 13.5 jit_solution(6301317189797041091)
XLA Ops:
  0.0 12.8 %shard_map.136 = bf16[1,1,160,512]{3,2,1,0:T(8,128)(2,1)S(1)} custom-call(bf16[1,1,1024,512]{3,2,1,0:T(8,128)(2,1)} %grid_h.1, bf16[1,1,160,512]{3,2,1,0:T(8,128)(2,1)} %mesh_h.1, f32[1,1,4,2048]{3,2,1,0:T(4,128)} %geo_h.1, s32[1,1,2048]{2,1,0:T(1,128)} %snd_h.1, s32[1,1,2048]{2,1,0:T(1,128)} %rcv_h.1, bf16[512,512]{1,0:T(8,128)(2,1)} %w_grid_h.1, ...), custom_call_target="tpu_custom_call" | custom-call | tf_op jit(solution)/shard_map/pallas_call | solution.py:406
  12.8 0.7 %copy.16 = bf16[1,1,160,512]{3,2,1,0:T(8,128)(2,1)} copy(bf16[1,1,160,512]{3,2,1,0:T(8,128)(2,1)S(1)} %shard_map.136) | data formatting | bytes 327680

commit v7 on v6

--- a/solution.py
+++ b/solution.py
@@ -20,7 +20,6 @@
 
 BF16 = jnp.bfloat16
 F32 = jnp.float32
-F8 = jnp.float8_e4m3fn
 
 SIDES = (1, 3, 5, 7)
 CORNERS = (0, 2, 6, 8)
@@ -85,7 +84,7 @@
     edge_table,
     low_v,
     high_v,
-    picks_8,
+    picks_v,
     before,
     put_sum,
     got_sum,
@@ -315,18 +314,15 @@
         for h in range(slots // LANES):
             found = equal(at, lanes[h])
             if h * LANES == cut:
-                twice = found.astype(F8)
-                picks_8[span, :] = jnp.concatenate([twice, twice], 1)
                 found = found + jnp.transpose(tail[:, start : start + step])
-            tiles.append(found)
-        before[span, :] = nn(jnp.concatenate(tiles, 1), table[...])
+            picks_v[span, pl.ds(h * LANES, LANES)] = found
+        before[span, :] = nn(jnp.concatenate(tiles, 1), table[:grid_rows, :])
 
     settle(strip_sem.at[1], 1)
 
-    arrived = edge_table[...].astype(F32)
-    rough = arrived.astype(F8)
-    fine = (arrived - rough.astype(F32)).astype(F8)
-    split = jnp.concatenate([rough, fine], 0)
+    first = grid_rows + rows
+    table[first:, :] = table[first:, :] + edge_table[rows - cut :, :]
+
     def gathered(first, count, begin, hidden):
         width = hidden.shape[0]
         row = lax.broadcasted_iota(jnp.int32, (count, width), 0) + first
@@ -340,7 +336,7 @@
     for number in range(len(sizes) + LAG):
         if number < len(sizes):
             span = pl.ds(begins[number], sizes[number])
-            half = before[span, :] + nn(picks_8[span, :], split)
+            half = before[span, :] + nn(picks_v[span, :], table[grid_rows:, :])
             halves_of.append(half)
         if 1 <= number <= len(sizes):
             half = halves_of[number - 1]
@@ -414,7 +410,7 @@
             pltpu.VMEM((slots - cut, features), BF16),
             pltpu.VMEM((edges, LANES), BF16),
             pltpu.VMEM((edges, LANES), BF16),
-            pltpu.VMEM((edges, 2 * LANES), F8),
+            pltpu.VMEM((edges, slots), BF16),
             pltpu.VMEM((edges, features), F32),
             pltpu.VMEM((slots - rows, features), BF16),
             pltpu.VMEM((slots - rows, features), BF16),

time: 13.7 us -> 13.7 us (level)
  no operation moved by 1% of the time
where the time goes in v7:
time: 13.7 us; the launch traced here: 13.5 us
  Pallas kernels  12.8 us (93%)
  local copies, waits for them, and re-layouts  0.67 us (5%)
    pallas_call x1, Pallas kernels, local(): pl.pallas_call(functools.partial(kernel, n_lon, n_lat), out_shape=pltpu.V...  12.8 us
    unnamed x1, local copies, waits for them, and re-layouts  0.67 us

profile of v7, /device:TPU:0, one launch (start us, length us, event | category | flops | bytes accessed | tf_op | source)
XLA Modules:
  0.0 13.5 jit_solution(5330937910638091685)
XLA Ops:
  0.0 12.8 %shard_map.136 = bf16[1,1,160,512]{3,2,1,0:T(8,128)(2,1)S(1)} custom-call(bf16[1,1,1024,512]{3,2,1,0:T(8,128)(2,1)} %grid_h.1, bf16[1,1,160,512]{3,2,1,0:T(8,128)(2,1)} %mesh_h.1, f32[1,1,4,2048]{3,2,1,0:T(4,128)} %geo_h.1, s32[1,1,2048]{2,1,0:T(1,128)} %snd_h.1, s32[1,1,2048]{2,1,0:T(1,128)} %rcv_h.1, bf16[512,512]{1,0:T(8,128)(2,1)} %w_grid_h.1, ...), custom_call_target="tpu_custom_call" | custom-call | tf_op jit(solution)/shard_map/pallas_call | solution.py:402
  12.8 0.7 %copy.16 = bf16[1,1,160,512]{3,2,1,0:T(8,128)(2,1)} copy(bf16[1,1,160,512]{3,2,1,0:T(8,128)(2,1)S(1)} %shard_map.136) | data formatting | bytes 327680
